TPU v7x, 32 devices: a whole 2x2x4 slice. The times are simulated.
32 devices in a mesh: site: 8 (over z, y), ka: 4 (over x, core).
Axes of the slice: x: 2, y: 2, z: 4, core: 2. Of those that a mesh axis runs over, the one named last changes fastest.
Arguments:
- positions: float32 [3, 128], P(None, 'site'), may hold values from 0 to 1
- site_class: int32 [128], P('site'), may hold values from 0 to 3
- class_charge: float32 [4], replicated, may hold values from -2 to 2
- miller: int32 [3, 524288], P(None, 'ka'), may hold values from -80 to 80, as said below
Outputs:
- forces: float32 [3, 128], P(None, ('site', 'ka'))
- energy: float32 [], replicated
Inputs may be any that keep to these rules, and one draw needn't show every extreme that they name: `miller`: the k-vectors are all distinct, and none has all three indices zero.
All inputs are finite; a program needn't handle non-finite values.
Results may differ from a plain program's by a relative error of at most 0.0003.
Values sent between devices are 32-bit elements; how exact they have to be, the bound alone decides.
A program may use at most 64 MiB of HBM per device.

v0:
```python
import math

import jax
import jax.numpy as jnp
from jax import lax
from jax.sharding import PartitionSpec as P

KBLOCK = 4096
MMAX = 80
NCLS = 4


def charges_of(site_class, class_charge):
    onehot = (site_class[None, :] == jnp.arange(NCLS, dtype=jnp.int32)[:, None]).astype(jnp.float32)
    return jnp.dot(class_charge, onehot, precision=lax.Precision.HIGHEST)


def kernel_weights(mfloat):
    square = jnp.sum(mfloat * mfloat, axis=0)
    limit = float(MMAX * MMAX)
    return limit * jnp.exp(-square / limit) / square


def phases(mblock, positions):
    angles = (
        2.0
        * math.pi
        * (
            mblock[0][:, None] * positions[0][None, :]
            + mblock[1][:, None] * positions[1][None, :]
            + mblock[2][:, None] * positions[2][None, :]
        )
    )
    return (jnp.cos(angles), jnp.sin(angles))


def force_terms(mblock, real_part, imag_part, wblock, cosine, sine):
    grad_sine = mblock * (wblock * real_part)[None, :]
    grad_cosine = mblock * (wblock * imag_part)[None, :]
    return jnp.dot(grad_sine, sine, precision=lax.Precision.HIGHEST) - jnp.dot(
        grad_cosine, cosine, precision=lax.Precision.HIGHEST
    )


def local(positions, site_class, class_charge, miller):
    local_sites = positions.shape[1]
    local_kvecs = miller.shape[1]
    nsites_all = local_sites * lax.axis_size("site")
    kvecs_all = local_kvecs * lax.axis_size("ka")
    charge = charges_of(site_class, class_charge)
    mfloat = miller.astype(jnp.float32)
    scale = 1.0 / math.sqrt(nsites_all)
    force_scale = 4.0 * math.pi / math.sqrt(nsites_all * kvecs_all)
    packed = jnp.concatenate([positions, charge[None, :]], axis=0)
    gathered = lax.all_gather(packed, "site", axis=1, tiled=True)
    all_positions = gathered[:3]
    all_charge = gathered[3]
    sub_count = local_kvecs // lax.axis_size("site")
    block_rows = KBLOCK // lax.axis_size("site")
    my_kvecs = lax.dynamic_slice_in_dim(mfloat, lax.axis_index("site") * sub_count, sub_count, 1)
    my_weights = kernel_weights(my_kvecs)
    nblocks = sub_count // block_rows
    my_blocks = my_kvecs.reshape(3, nblocks, block_rows).transpose(1, 0, 2)
    my_wblocks = my_weights.reshape(nblocks, block_rows)

    def gather_step(total, items):
        mblock, wblock = items
        cosine, sine = phases(mblock, all_positions)
        real_part = jnp.dot(cosine, all_charge, precision=lax.Precision.HIGHEST) * scale
        imag_part = jnp.dot(sine, all_charge, precision=lax.Precision.HIGHEST) * scale
        total = total + force_terms(mblock, real_part, imag_part, wblock, cosine, sine)
        return (total, jnp.sum(wblock * (real_part * real_part + imag_part * imag_part)))

    total, energy_terms = lax.scan(
        gather_step, jnp.zeros((3, nsites_all), jnp.float32), (my_blocks, my_wblocks)
    )
    forces_local = force_scale * all_charge[None, :] * total
    forces = lax.psum_scatter(forces_local, ("site", "ka"), scatter_dimension=1, tiled=True)
    energy_sum = lax.psum(jnp.sum(energy_terms), ("site", "ka"))
    return (forces, energy_sum / kvecs_all)


def solution(mesh):
    placed = (P(None, "site"), P("site"), P(), P(None, "ka"))
    return jax.shard_map(
        local, mesh=mesh, in_specs=placed, out_specs=(P(None, ("site", "ka")), P()), check_vma=False
    )
```

profile of v0, /device:TPU:0, one launch (start us, length us, event | category | flops | bytes accessed | tf_op | source)
XLA Modules:
  0.0 283.3 jit_solution(1043743584473158097)
XLA Ops:
  3.3 27.9 %all-gather = f32[8,16,4]{1,2,0:T(4,128)S(1)} all-gather(f32[1,16,4]{1,2,0:T(4,128)S(1)} %maximum_bitcast_fusion), channel_id=1, replica_groups=mesh['site'=8,'ka'=4] {'site'}, dimensions={0}, use_global_device_ids=true | all-gather | bytes 2304 | tf_op jit(solution)/shard_map/all_gather | solution.py:55
  31.4 209.8 %while.13 = (s32[]{:T(128)}, f32[3,128]{1,0:T(4,128)S(1)}, f32[32]{0:T(128)S(1)}, f32[32,3,512]{2,1,0:T(4,128)S(1)}, f32[32,512]{1,0:T(8,128)S(1)}, /*index=5*/f...) while((s32[]{:T(128)}, f32[3,128]{1,0:T(4,128)S(1)}, ...), condition=%wide.region_3.4_spmd.clone, body=%wide.region_1.3_spmd.clone.sunk | while | flops 7873156 | bytes 93367 | solution.py:74
  31.4 1.3 fusion.70
  32.7 1.3 fusion.69
  38.0 1.3 fusion.70
  39.3 1.3 fusion.69
  44.5 1.3 fusion.70
  45.8 1.3 fusion.69
  51.1 1.3 fusion.70
  52.4 1.3 fusion.69
  57.6 1.3 fusion.70
  58.9 1.3 fusion.69
  64.2 1.3 fusion.70
  65.5 1.3 fusion.69
  70.7 1.3 fusion.70
  72.0 1.3 fusion.69
  77.3 1.3 fusion.70
  78.6 1.3 fusion.69
  83.8 1.3 fusion.70
  85.2 1.3 fusion.69
  90.4 1.3 fusion.70
  91.7 1.3 fusion.69
  97.0 1.3 fusion.70
  98.3 1.3 fusion.69
  103.5 1.3 fusion.70
  104.8 1.3 fusion.69
  110.1 1.3 fusion.70
  111.4 1.3 fusion.69
  116.6 1.3 fusion.70
  117.9 1.3 fusion.69
  123.2 1.3 fusion.70
  124.5 1.3 fusion.69
  129.7 1.3 fusion.70
  131.0 1.3 fusion.69
  136.3 1.3 fusion.70
  137.6 1.3 fusion.69
  142.8 1.3 fusion.70
  144.1 1.3 fusion.69
  149.4 1.3 fusion.70
  150.7 1.3 fusion.69
  155.9 1.3 fusion.70
  157.3 1.3 fusion.69
  162.5 1.3 fusion.70
  163.8 1.3 fusion.69
  169.1 1.3 fusion.70
  170.4 1.3 fusion.69
  175.6 1.3 fusion.70
  176.9 1.3 fusion.69
  183.5 1.3 fusion.69
  190.0 1.3 fusion.69
  195.3 1.3 fusion.70
  196.6 1.3 fusion.69
  201.8 1.3 fusion.70
  203.1 1.3 fusion.69
  208.4 1.3 fusion.70
  209.7 1.3 fusion.69
  214.9 1.3 fusion.70
  216.2 1.3 fusion.69
  221.5 1.3 fusion.70
  222.8 1.3 fusion.69
  229.4 1.3 fusion.69
  234.6 1.3 fusion.70
  235.9 1.3 fusion.69
  241.7 39.1 %all-reduce.1 = (f32[3,128]{1,0:T(4,128)S(1)}, f32[]{:T(128)}) all-reduce(f32[3,128]{1,0:T(4,128)S(1)} %broadcast_multiply_fusion, f32[]{:T(128)} %reduce_sum.31), channel_id=2, replica_groups=mesh['site'=8,'ka'=4] {'site','ka'}, use_global_device_ids=true, to_apply=%region_4.5.clone | all-reduce | flops 385 | bytes 3080
  (242 shorter events, 131.7 us)
Async XLA Ops:
  0.6 1.2 copy-start
where the time goes:
time: 284 us; the launch traced here: 283 us
  matrix products  164 us (58%)
  blocking collectives  67 us (24%)
  local copies, waits for them, and re-layouts  26.6 us (9%)
  other arithmetic  21.8 us (8%)
    dot_general x32, matrix products, gather_step(): jnp.dot(sine, all_charge, precision=lax.Precision.HIGHEST) * scale  42.9 us
    dot_general x32, matrix products, gather_step(): jnp.dot(cosine, all_charge, precision=lax.Precision.HIGHEST) * scale  41.9 us
    dot_general x32, matrix products, force_terms(): jnp.dot(grad_cosine, cosine, precision=lax.Precision.HIGHEST)  39.5 us
    unnamed x1, blocking collectives  39.1 us
    dot_general x32, matrix products, force_terms(): jnp.dot(grad_sine, sine, precision=lax.Precision.HIGHEST)  39.1 us
    all_gather x1, blocking collectives, local(): gathered = lax.all_gather(packed, 'site', axis=1, tiled=True)  27.9 us
    dynamic_update_slice x32, local copies, waits for them, and re-layouts, local(): lax.scan(gather_step, jnp.zeros((3, nsites_all), jnp.float32), (my_blocks...  24.7 us
    reduce_sum x32, other arithmetic, gather_step(): jnp.sum(wblock * (real_part * real_part + imag_part * imag_part))  19.4 us

commit v1 on v0

v1 whole, which is shorter than its diff:
```python
import functools
import math

import jax
import jax.numpy as jnp
from jax import lax
from jax.experimental import pallas as pl
from jax.experimental.pallas import tpu as pltpu
from jax.sharding import PartitionSpec as P

MMAX = 80
NCLS = 4
MESH = pl.DeviceIdType.MESH
F32 = jnp.float32
BF16 = jnp.bfloat16
A0, A1, A2 = 1.5707884689227576, -0.645711988911062, 0.07766738858001387
TINY = 1e-24
KB = 512
ROWS = 16


def kernel(
    nsite, nka, nsites, kvecs,
    pos_ref, cls_ref, cc_ref, mil_ref,
    out_ref, en_ref,
    mi, m16, wts, x16, alpha2, ca0, ca1, ca2, qabs, sh, ch, vbuf, facc, eacc, qtot,
    ag_out, ag_in, rs_out, rs_in,
    mil_sem, ag_send, ag_recv, rs_send, rs_recv,
):
    ndev = nsite * nka
    si, ki = lax.axis_index("site"), lax.axis_index("ka")
    me = si * nka + ki
    ls = pos_ref.shape[1]
    sub = mi.shape[1]
    spd = nsites // ndev
    nblk = sub // KB

    mil_copy = pltpu.make_async_copy(
        mil_ref.at[:, pl.ds(pl.multiple_of(si * sub, 128), sub)], mi, mil_sem
    )
    mil_copy.start()

    cls = cls_ref[...]
    charge = jnp.zeros(cls.shape, F32)
    for c in range(NCLS):
        charge = jnp.where(cls == c, cc_ref[c], charge)
    ag_out[...] = jnp.zeros_like(ag_out)
    ag_out[0:3, 0:ls] = pos_ref[...]
    ag_out[3:4, 0:ls] = charge

    barrier = pltpu.get_barrier_semaphore()

    @pl.loop(1, ndev)
    def _(i):
        to = lax.rem(me + i, ndev)
        pl.semaphore_signal(
            barrier, inc=1, device_id=(lax.div(to, nka), lax.rem(to, nka)), device_id_type=MESH
        )

    mil_copy.wait()

    @pl.loop(0, nblk)
    def _(b):
        at = pl.ds(pl.multiple_of(b * KB, KB), KB)
        m = mi[:, at].astype(F32)
        sq = jnp.sum(m * m, axis=0, keepdims=True)
        limit = float(MMAX * MMAX)
        wts[:, at] = limit * jnp.exp(sq * (-1.0 / limit)) / sq
        m16[:, at] = jnp.concatenate(
            [m, m, m, jnp.ones((1, KB), F32), jnp.zeros((6, KB), F32)], axis=0
        ).astype(BF16)

    pl.semaphore_wait(barrier, ndev - 1)

    def ag_copy(src, to):
        return pltpu.make_async_remote_copy(
            src_ref=ag_out, dst_ref=ag_in.at[src], send_sem=ag_send.at[to],
            recv_sem=ag_recv.at[src], device_id=(to, ki), device_id_type=MESH,
        )

    @pl.loop(1, nsite)
    def _(i):
        ag_copy(si, lax.rem(si + i, nsite)).start()

    ag_in[si] = ag_out[...]

    @pl.loop(1, nsite)
    def _(i):
        other = lax.rem(si + i, nsite)
        ag_copy(other, other).wait_recv()

    per = 128 // ls
    for t in range(nsites // 128):
        allrows = ag_in[t * per]
        for i in range(1, per):
            allrows = allrows + pltpu.roll(ag_in[t * per + i], i * ls, 1)
        x = allrows[0:3]
        x = x - jnp.round(x)
        q = allrows[3:4]
        x1 = x.astype(BF16).astype(F32)
        x2 = (x - x1).astype(BF16).astype(F32)
        x3 = x - x1 - x2
        half = jnp.where(q < 0.0, 0.5, 0.0)
        qc = jnp.maximum(jnp.abs(q), TINY)
        al2 = jnp.sqrt(qc)
        al = jnp.sqrt(al2)
        rows = jnp.concatenate(
            [x1, x2, x3, half, al2, al * A0, al * A1, al * A2, jnp.abs(q), qc,
             jnp.zeros((112, 128), F32)], axis=0
        )
        cols = rows.T
        rs_ = pl.ds(t * 128, 128)
        x16[rs_, :] = cols[:, 0:16].astype(BF16)
        alpha2[rs_, :] = jnp.broadcast_to(cols[:, 10:11], (128, 128))
        ca0[rs_, :] = jnp.broadcast_to(cols[:, 11:12], (128, 128))
        ca1[rs_, :] = jnp.broadcast_to(cols[:, 12:13], (128, 128))
        ca2[rs_, :] = jnp.broadcast_to(cols[:, 13:14], (128, 128))
        qabs[rs_, 0:2] = cols[:, 14:16]
        total = jnp.broadcast_to(jnp.sum(qc, axis=1, keepdims=True), (1, 128))
        qtot[...] = total if t == 0 else qtot[...] + total

    facc[...] = jnp.zeros_like(facc)
    eacc[...] = jnp.zeros_like(eacc)
    isn = 1.0 / math.sqrt(nsites)

    def wide(v):
        return jnp.concatenate([v] * (KB // 128), axis=1)

    @pl.loop(0, nblk)
    def _(b):
        at = pl.ds(pl.multiple_of(b * KB, KB), KB)
        mb = m16[:, at]
        turns = jnp.dot(x16[...], mb, preferred_element_type=F32)
        sums = sumc = None
        for j in range(nsites // ROWS):
            rr = slice(j * ROWS, (j + 1) * ROWS)
            t = turns[rr]
            r = t - jnp.round(t)
            z = r * r
            s = r * (wide(ca0[rr]) + z * (wide(ca1[rr]) + z * wide(ca2[rr])))
            s2 = s * s
            u = wide(alpha2[rr]) - s2
            sc = s * (u * lax.rsqrt(u))
            dc = u - s2
            sj = sc * dc
            cj = sc * sc
            sh[rr] = sj
            ch[rr] = cj
            sums = sj if j == 0 else sums + sj
            sumc = cj if j == 0 else sumc + cj
        cimag = (4.0 * isn) * jnp.sum(sums, axis=0, keepdims=True)
        creal = isn * (wide(qtot[...]) - 8.0 * jnp.sum(sumc, axis=0, keepdims=True))
        w = wts[:, at]
        g1 = w * creal
        g2 = w * cimag
        eacc[...] += g1 * creal + g2 * cimag
        g2 = 2.0 * g2

        def split(v, rows):
            hi = v.astype(BF16)
            vbuf[rows, 0:KB] = hi
            vbuf[rows, KB:] = (v - hi.astype(F32)).astype(BF16)

        for j in range(nsites // ROWS):
            rr = slice(j * ROWS, (j + 1) * ROWS)
            split(sh[rr] * g1 + ch[rr] * g2, rr)
        split(jnp.broadcast_to(g2, (ROWS, KB)), slice(nsites, nsites + ROWS))
        facc[...] += lax.dot_general(
            vbuf[...], jnp.concatenate([mb, mb], axis=1), (((1,), (1,)), ((), ())),
            preferred_element_type=F32,
        )

    energy = jnp.sum(eacc[...], axis=1, keepdims=True) * (1.0 / kvecs)
    fscale = 4.0 * math.pi / math.sqrt(nsites * kvecs)
    qa, qc = qabs[:, 0:1], qabs[:, 1:2]
    forces = (fscale * (qa / qc)) * (4.0 * facc[0:nsites] - (0.5 * qc) * facc[nsites : nsites + 1])
    lane = lax.broadcasted_iota(jnp.int32, forces.shape, 1)
    forces = jnp.where(lane == 3, energy, forces)
    rs_out[...] = jnp.zeros_like(rs_out)
    for p in range(ndev):
        rs_out[p, :, 0:16] = forces[p * spd : (p + 1) * spd]

    def rs_copy(src, to):
        return pltpu.make_async_remote_copy(
            src_ref=rs_out.at[to], dst_ref=rs_in.at[src], send_sem=rs_send.at[to],
            recv_sem=rs_recv.at[src], device_id=(lax.div(to, nka), lax.rem(to, nka)),
            device_id_type=MESH,
        )

    @pl.loop(1, ndev)
    def _(i):
        rs_copy(me, lax.rem(me + i, ndev)).start()

    rs_in[me] = rs_out[me]

    @pl.loop(1, ndev)
    def _(i):
        other = lax.rem(me + i, ndev)
        rs_copy(other, me).wait_recv()

    mine = jnp.sum(rs_in[...], axis=0)
    sub_i = lax.broadcasted_iota(jnp.int32, (spd, 128), 0)
    lane_i = lax.broadcasted_iota(jnp.int32, (spd, 128), 1)
    for d in range(3):
        row = jnp.sum(jnp.where(sub_i == lane_i, mine[:, d : d + 1], 0.0), axis=0, keepdims=True)
        out_ref[d : d + 1, :] = row[:, 0:spd]
    en_ref[...] = mine[0:1, 3:4]

    @pl.loop(1, ndev)
    def _(i):
        rs_copy(me, lax.rem(me + i, ndev)).wait_send()

    @pl.loop(1, nsite)
    def _(i):
        ag_copy(si, lax.rem(si + i, nsite)).wait_send()


def local(nsite, nka, positions, site_class, class_charge, miller):
    ndev = nsite * nka
    ls = positions.shape[1]
    nsites = ls * nsite
    kvecs = miller.shape[1] * nka
    sub = miller.shape[1] // nsite
    spd = nsites // ndev
    vmem = pl.BlockSpec(memory_space=pltpu.VMEM)
    forces, energy = pl.pallas_call(
        functools.partial(kernel, nsite, nka, nsites, kvecs),
        out_shape=(jax.ShapeDtypeStruct((3, spd), F32), jax.ShapeDtypeStruct((1, 1), F32)),
        in_specs=[
            vmem, vmem, pl.BlockSpec(memory_space=pltpu.SMEM), pl.BlockSpec(memory_space=pl.ANY),
        ],
        out_specs=(vmem, vmem),
        scratch_shapes=[
            pltpu.VMEM((3, sub), jnp.int32),
            pltpu.VMEM((16, sub), BF16),
            pltpu.VMEM((1, sub), F32),
            pltpu.VMEM((nsites, 16), BF16),
            pltpu.VMEM((nsites, 128), F32),
            pltpu.VMEM((nsites, 128), F32),
            pltpu.VMEM((nsites, 128), F32),
            pltpu.VMEM((nsites, 128), F32),
            pltpu.VMEM((nsites, 128), F32),
            pltpu.VMEM((nsites, KB), F32),
            pltpu.VMEM((nsites, KB), F32),
            pltpu.VMEM((nsites + ROWS, 2 * KB), BF16),
            pltpu.VMEM((nsites + ROWS, 16), F32),
            pltpu.VMEM((1, KB), F32),
            pltpu.VMEM((1, 128), F32),
            pltpu.VMEM((8, 128), F32),
            pltpu.VMEM((nsite, 8, 128), F32),
            pltpu.VMEM((ndev, spd, 128), F32),
            pltpu.VMEM((ndev, spd, 128), F32),
            pltpu.SemaphoreType.DMA,
            pltpu.SemaphoreType.DMA((nsite,)),
            pltpu.SemaphoreType.DMA((nsite,)),
            pltpu.SemaphoreType.DMA((ndev,)),
            pltpu.SemaphoreType.DMA((ndev,)),
        ],
        compiler_params=pltpu.CompilerParams(collective_id=0, has_side_effects=True),
        name="ewald",
    )(positions, site_class.reshape(1, ls), class_charge, miller)
    return forces, energy[0, 0]


def solution(mesh):
    placed = (P(None, "site"), P("site"), P(), P(None, "ka"))
    return jax.shard_map(
        functools.partial(local, mesh.shape["site"], mesh.shape["ka"]),
        mesh=mesh,
        in_specs=placed,
        out_specs=(P(None, ("site", "ka")), P()),
        check_vma=False,
    )
```

time: 284 us -> 39 us (0.14)
  matrix products: 164 us -> 0 us
  blocking collectives: 67 us -> 0 us
  Pallas kernels: 0 us -> 35.1 us
  local copies, waits for them, and re-layouts: 26.6 us -> 1.25 us
  other arithmetic: 21.8 us -> 0 us
    dot_general x129 -> x0, matrix products: 164 us -> none  [the longest x32 42.9 us: gather_step(): jnp.dot(sine, all_charge, precision=lax.Precision.HIGHEST) * scale]
    unnamed x1 -> x0, blocking collectives: 39.1 us -> none
    pallas_call x0 -> x1, Pallas kernels: none -> 35.1 us  [local(): pl.pallas_call(functools.partial(kernel, nsite, nka, nsites, kvecs), out_...]
    all_gather x1 -> x0, blocking collectives: 27.9 us -> none  [local(): gathered = lax.all_gather(packed, 'site', axis=1, tiled=True)]
    dynamic_update_slice x32 -> x0, local copies, waits for them, and re-layouts: 24.7 us -> none  [local(): lax.scan(gather_step, jnp.zeros((3, nsites_all), jnp.float32), (my_blocks...]
    reduce_sum x34 -> x0, other arithmetic: 21.1 us -> none  [the longest x32 19.4 us: gather_step(): jnp.sum(wblock * (real_part * real_part + imag_part * imag_part))]
where the time goes in v1:
time: 39 us; the launch traced here: 38.8 us
  Pallas kernels  35.1 us (90%)
  between operations  2.4 us (6%)
  local copies, waits for them, and re-layouts  1.25 us (3%)
    pallas_call x1, Pallas kernels, local(): pl.pallas_call(functools.partial(kernel, nsite, nka, nsites, kvecs), out_...  35.1 us
    unnamed x1, local copies, waits for them, and re-layouts  1.25 us

profile of v1, /device:TPU:0, one launch (start us, length us, event | category | flops | bytes accessed | tf_op | source)
XLA Modules:
  0.0 38.8 jit_solution(3607690588455985305)
XLA Ops:
  0.6 35.1 %ewald.1 = (f32[3,4]{1,0:T(4,128)}, f32[1,1]{1,0:T(1,128)}) custom-call(f32[3,16]{1,0:T(4,128)} %pos_ref.1, s32[1,16]{1,0:T(1,128)} %bitcast.2, f32[4]{0:T(128)} %cc_ref.1, s32[3,131072]{1,0:T(4,128)} %mil_ref.1), custom_call_target="tpu_custom_call" | custom-call | tf_op jit(solution)/shard_map/ewald/pallas_call | solution.py:226
  35.8 1.2 %copy.8 = f32[3,4]{1,0:T(4,128)} copy(f32[3,4]{1,0:T(4,128)} %get-tuple-element.8) | data formatting | bytes 96

commit v2 on v1

--- a/solution.py
+++ b/solution.py
@@ -23,7 +23,7 @@
     nsite, nka, nsites, kvecs,
     pos_ref, cls_ref, cc_ref, mil_ref,
     out_ref, en_ref,
-    mi, m16, wts, x16, alpha2, ca0, ca1, ca2, qabs, sh, ch, vbuf, facc, eacc, qtot,
+    mi, m16, wts, x16, alpha2, ca0, ca1, ca2, qabs, sh, ch, vbuf, facc, eacc, qtot, tbuf, gr1, gr2,
     ag_out, ag_in, rs_out, rs_in,
     mil_sem, ag_send, ag_recv, rs_send, rs_recv,
 ):
@@ -126,15 +126,40 @@
     def wide(v):
         return jnp.concatenate([v] * (KB // 128), axis=1)
 
+    def cols_of(b):
+        return pl.ds(pl.multiple_of(b * KB, KB), KB)
+
+    def split(v, rows):
+        hi = v.astype(BF16)
+        vbuf[rows, 0:KB] = hi
+        vbuf[rows, KB:] = (v - hi.astype(F32)).astype(BF16)
+
+    def gather_forces(b):
+        mb = m16[:, cols_of(b)]
+        facc[...] += lax.dot_general(
+            vbuf[...], jnp.concatenate([mb, mb], axis=1), (((1,), (1,)), ((), ())),
+            preferred_element_type=F32,
+        )
+
+    def second(rr):
+        split(sh[rr] * gr1[...] + ch[rr] * gr2[...], rr)
+
+    extra = slice(nsites, nsites + ROWS)
+    chunks = [slice(j * ROWS, (j + 1) * ROWS) for j in range(nsites // ROWS)]
+    for buf in (sh, ch, gr1, gr2, vbuf):
+        buf[...] = jnp.zeros_like(buf)
+    tbuf[...] = jnp.dot(x16[...], m16[:, 0:KB], preferred_element_type=F32)
+
     @pl.loop(0, nblk)
     def _(b):
-        at = pl.ds(pl.multiple_of(b * KB, KB), KB)
-        mb = m16[:, at]
-        turns = jnp.dot(x16[...], mb, preferred_element_type=F32)
+        gather_forces(jnp.maximum(b - 2, 0))
+        turns = jnp.dot(
+            x16[...], m16[:, cols_of(jnp.minimum(b + 1, nblk - 1))], preferred_element_type=F32
+        )
         sums = sumc = None
-        for j in range(nsites // ROWS):
-            rr = slice(j * ROWS, (j + 1) * ROWS)
-            t = turns[rr]
+        for j, rr in enumerate(chunks):
+            second(rr)
+            t = tbuf[rr]
             r = t - jnp.round(t)
             z = r * r
             s = r * (wide(ca0[rr]) + z * (wide(ca1[rr]) + z * wide(ca2[rr])))
@@ -146,29 +171,24 @@
             cj = sc * sc
             sh[rr] = sj
             ch[rr] = cj
+            tbuf[rr] = turns[rr]
             sums = sj if j == 0 else sums + sj
             sumc = cj if j == 0 else sumc + cj
+        split(jnp.broadcast_to(gr2[...], (ROWS, KB)), extra)
         cimag = (4.0 * isn) * jnp.sum(sums, axis=0, keepdims=True)
         creal = isn * (wide(qtot[...]) - 8.0 * jnp.sum(sumc, axis=0, keepdims=True))
-        w = wts[:, at]
+        w = wts[:, cols_of(b)]
         g1 = w * creal
         g2 = w * cimag
         eacc[...] += g1 * creal + g2 * cimag
-        g2 = 2.0 * g2
-
-        def split(v, rows):
-            hi = v.astype(BF16)
-            vbuf[rows, 0:KB] = hi
-            vbuf[rows, KB:] = (v - hi.astype(F32)).astype(BF16)
-
-        for j in range(nsites // ROWS):
-            rr = slice(j * ROWS, (j + 1) * ROWS)
-            split(sh[rr] * g1 + ch[rr] * g2, rr)
-        split(jnp.broadcast_to(g2, (ROWS, KB)), slice(nsites, nsites + ROWS))
-        facc[...] += lax.dot_general(
-            vbuf[...], jnp.concatenate([mb, mb], axis=1), (((1,), (1,)), ((), ())),
-            preferred_element_type=F32,
-        )
+        gr1[...] = g1
+        gr2[...] = 2.0 * g2
+
+    gather_forces(max(nblk - 2, 0))
+    for rr in chunks:
+        second(rr)
+    split(jnp.broadcast_to(gr2[...], (ROWS, KB)), extra)
+    gather_forces(nblk - 1)
 
     energy = jnp.sum(eacc[...], axis=1, keepdims=True) * (1.0 / kvecs)
     fscale = 4.0 * math.pi / math.sqrt(nsites * kvecs)
@@ -246,6 +266,9 @@
             pltpu.VMEM((nsites + ROWS, 16), F32),
             pltpu.VMEM((1, KB), F32),
             pltpu.VMEM((1, 128), F32),
+            pltpu.VMEM((nsites, KB), F32),
+            pltpu.VMEM((1, KB), F32),
+            pltpu.VMEM((1, KB), F32),
             pltpu.VMEM((8, 128), F32),
             pltpu.VMEM((nsite, 8, 128), F32),
             pltpu.VMEM((ndev, spd, 128), F32),

time: 39 us -> 33.4 us (0.86)
  Pallas kernels: 35.1 us -> 29.5 us
    pallas_call x1, Pallas kernels: 35.1 us -> 29.5 us  [local(): pl.pallas_call(functools.partial(kernel, nsite, nka, nsites, kvecs), out_...]
where the time goes in v2:
time: 33.4 us; the launch traced here: 33.1 us
  Pallas kernels  29.5 us (88%)
  between operations  2.4 us (7%)
  local copies, waits for them, and re-layouts  1.25 us (4%)
    pallas_call x1, Pallas kernels, local(): pl.pallas_call(functools.partial(kernel, nsite, nka, nsites, kvecs), out_...  29.5 us
    unnamed x1, local copies, waits for them, and re-layouts  1.25 us

profile of v2, /device:TPU:0, one launch (start us, length us, event | category | flops | bytes accessed | tf_op | source)
XLA Modules:
  0.0 33.1 jit_solution(824961050059176871)
XLA Ops:
  0.6 29.5 %ewald.1 = (f32[3,4]{1,0:T(4,128)}, f32[1,1]{1,0:T(1,128)}) custom-call(f32[3,16]{1,0:T(4,128)} %pos_ref.1, s32[1,16]{1,0:T(1,128)} %bitcast.2, f32[4]{0:T(128)} %cc_ref.1, s32[3,131072]{1,0:T(4,128)} %mil_ref.1), custom_call_target="tpu_custom_call" | custom-call | tf_op jit(solution)/shard_map/ewald/pallas_call | solution.py:246
  30.1 1.2 %copy.8 = f32[3,4]{1,0:T(4,128)} copy(f32[3,4]{1,0:T(4,128)} %get-tuple-element.8) | data formatting | bytes 96
